TPU v7x, 32 devices: a whole 2x2x4 slice. The times are simulated.
32 devices in a mesh: group: 8 (over z, x), tensor: 4 (over y, core).
Axes of the slice: x: 2, y: 2, z: 4, core: 2. Of those that a mesh axis runs over, the one named last changes fastest.
Arguments:
- queries: bfloat16 [64, 64, 5120], P('group', None, 'tensor'), may hold values from -15 to 15
- prefix_keys: bfloat16 [16, 1024, 1024], P('group', None, 'tensor'), may hold values from -200 to 200
- prefix_values: bfloat16 [16, 1024, 1024], P('group', None, 'tensor'), may hold values from -6 to 6
- slot_of_prompt: int32 [16], replicated, may hold values from 0 to 15, as said below
- prompt_of: int32 [64], P('group'), may hold values from 0 to 15, as said below
- lengths: int32 [64], P('group'), may hold values from 1 to 64
Outputs:
- attended: bfloat16 [64, 64, 5120], P('group', 'tensor')
Inputs may be any that keep to these rules, and one draw needn't show every extreme that they name: A permutation: prompt p's keys and values lie in row slot_of_prompt[p] of the prefix arrays, and that row belongs to group index slot_of_prompt[p] // 2. `prompt_of`: of the 8 completions on one group index, at most 2 have prompts cached on any one group index, and on every group index some group index caches the prompts of exactly 2 of them.
All inputs are finite; a program needn't handle non-finite values.
Results may differ from a plain program's by a relative error of at most 0.012.
Values may be sent and summed in bfloat16 or wider, within the bound.
A program may use at most 128 MiB of HBM per device.

v0:
```python
import functools
import math

import numpy as np

import jax
import jax.numpy as jnp
from jax import lax
from jax.experimental import pallas as pl
from jax.experimental.pallas import tpu as pltpu
from jax.sharding import PartitionSpec as P

HEAD = 128
CAPC = 2
ROTARY_BASE = 1000000.0
TILE = 16
MESH = pl.DeviceIdType.MESH


def rotary_tables(first_position, rows):
    half = HEAD // 2
    frequencies = np.float32(ROTARY_BASE) ** (
        -(np.arange(half, dtype=np.float32) * np.float32(2.0) / np.float32(HEAD))
    )
    positions = (first_position + np.arange(rows)).astype(np.float32)
    angles = (positions[:, None] * frequencies.astype(np.float32)[None, :]).astype(np.float64)
    cos, sin = np.cos(angles), np.sin(angles)
    return (
        np.concatenate([cos, cos], axis=1).astype(np.float32),
        np.concatenate([-sin, sin], axis=1).astype(np.float32),
    )


def kernel(
    groups, lanes, moved,
    source_ref, tag_ref, dest_ref, length_ref,
    q_ref, k_ref, v_ref, cos_ref, sin_ref,
    out_ref,
    q_out, q_in, sel_out, sel_in, res, stage,
    q_send, q_recv, s_send, s_recv, r_send, r_recv,
    *near,
):
    me, lane = lax.axis_index("group"), lax.axis_index("tensor")
    held, rows, width = q_ref.shape
    cached, prefix, kv_width = k_ref.shape
    share = rows // lanes
    kv_local = kv_width // HEAD
    per_kv = width // HEAD // kv_local
    half = groups // 2
    factor = math.log2(math.e) / math.sqrt(HEAD)
    wide_near = moved * per_kv * HEAD
    if moved:
        (n_out, n_in, ns_out, ns_in, n_res, k_far, v_far,
         n_send, n_recv, ns_send, ns_recv, nr_send, nr_recv, kv_send, kv_recv) = near
    spot = lax.rem(me, half)
    base = me - spot
    mirror = lax.rem(me + half, groups)

    barrier = pltpu.get_barrier_semaphore()

    def greet(step, carry):
        for turn in range(lanes):
            def send():
                pl.semaphore_signal(
                    barrier, inc=1,
                    device_id=(lax.rem(me + step, groups), lax.rem(lane + turn, lanes)),
                    device_id_type=MESH,
                )
            if turn:
                send()
            else:
                pl.when(step > 0)(send)
        return carry

    lax.fori_loop(0, groups, greet, 0)

    def offset_of(step):
        swing = (step + 1) // 2
        return lax.rem(half + (1 - 2 * lax.rem(step, 2)) * swing + groups, groups)

    def route(owner):
        places = [owner * CAPC + slot for slot in range(CAPC)]
        return [(source_ref[place], tag_ref[place]) for place in places]

    def fill(items, q_to, sel_to, block, first, last):
        for slot, (item, tag) in enumerate(items):
            for j in range(cached):
                weight = jnp.where(tag == j, 1.0, 0.0)
                sel_to[block, slot * cached + j] = jnp.full(
                    (TILE, HEAD), weight, jnp.float32
                ).astype(jnp.bfloat16)
            for head in range(first, last):
                x = q_ref[item, :, head * HEAD:(head + 1) * HEAD].astype(jnp.float32)
                turned = x * cos_ref[...] + pltpu.roll(x, HEAD // 2, 1) * sin_ref[...]
                span = slice((head - first) * HEAD, (head - first + 1) * HEAD)
                q_to[block, slot, :, span] = turned.astype(jnp.bfloat16)

    near_heads, all_heads = moved * per_kv, width // HEAD

    def pair(src, dst, send_sem, recv_sem, device):
        return pltpu.make_async_remote_copy(
            src_ref=src, dst_ref=dst, send_sem=send_sem, recv_sem=recv_sem,
            device_id=device, device_id_type=MESH,
        )

    def q_copies(here, there, device):
        return (
            pair(sel_out.at[here], sel_in.at[there], s_send.at[here], s_recv.at[there],
                 (device, lane)),
            pair(q_out.at[here], q_in.at[there], q_send.at[here], q_recv.at[there],
                 (device, lane)),
        )

    def n_copies(here, there, device):
        return (
            pair(ns_out.at[here], ns_in.at[there], ns_send.at[here], ns_recv.at[there],
                 (device, lane)),
            pair(n_out.at[here], n_in.at[there], n_send.at[here], n_recv.at[there],
                 (device, lane)),
        )

    def place(owner, from_lane, skip, wide):
        start = pl.multiple_of(from_lane * width + skip, HEAD)
        return stage.at[pl.ds(owner * CAPC, CAPC), :, pl.ds(start, wide)]

    def r_copy(block, piece, owner, from_lane, device):
        return pair(
            res.at[block, :, piece], place(owner, from_lane, wide_near, width - wide_near),
            r_send.at[block, piece], r_recv.at[owner, from_lane], (device, piece),
        )

    def nr_copy(block, piece, owner, from_lane, device):
        return pair(
            n_res.at[block, :, piece], place(owner, from_lane, 0, wide_near),
            nr_send.at[block, piece], nr_recv.at[owner, from_lane], (device, piece),
        )

    def kv_copies():
        span = pl.ds(0, moved * HEAD)
        return (
            pair(k_ref.at[:, :, span], k_far, kv_send.at[0], kv_recv.at[0], (mirror, lane)),
            pair(v_ref.at[:, :, span], v_far, kv_send.at[1], kv_recv.at[1], (mirror, lane)),
        )

    items = route(mirror)
    fill(items, q_out, sel_out, mirror, near_heads, all_heads)
    pl.semaphore_wait(barrier, groups * lanes - 1)
    for copy in q_copies(mirror, me, mirror):
        copy.start()
    if moved:
        fill(items, n_in, ns_in, spot + half, 0, near_heads)

    def dispatch(step, carry):
        owner = lax.rem(me + offset_of(step), groups)
        items = route(owner)
        fill(items, q_out, sel_out, owner, near_heads, all_heads)
        for copy in q_copies(owner, me, owner):
            copy.start()
        if moved:
            fill(items, n_out, ns_out, owner, 0, near_heads)
            seat = lax.rem(owner, half)
            kind = lax.rem(lax.div(owner, half) + lax.div(me, half), 2)
            for copy in n_copies(owner, spot + half * kind, base + seat):
                copy.start()
        return carry

    lax.fori_loop(1, groups - 1, dispatch, 0)
    if moved:
        for copy in kv_copies():
            copy.start()
    items = route(me)
    fill(items, q_in, sel_in, me, near_heads, all_heads)
    if moved:
        fill(items, n_in, ns_in, spot, 0, near_heads)

    def attend(q_from, sel_from, to, block, keys, values, first, count):
        for slot in range(CAPC):
            weights = [sel_from[block, slot * cached + j][None] for j in range(cached)]

            def chosen(ref, span):
                total = None
                for j in range(cached):
                    part = ref[j, :, span].reshape(prefix // TILE, TILE, HEAD) * weights[j]
                    total = part if total is None else total + part
                return total.reshape(prefix, HEAD)

            for kv in range(count):
                span = slice((first + kv) * HEAD, (first + kv + 1) * HEAD)
                spans = [
                    slice((kv * per_kv + g) * HEAD, (kv * per_kv + g + 1) * HEAD)
                    for g in range(per_kv)
                ]
                query = jnp.concatenate([q_from[block, slot, :, s] for s in spans], axis=0)
                scores = lax.dot_general(
                    query, chosen(keys, span), (((1,), (1,)), ((), ())),
                    preferred_element_type=jnp.float32,
                )
                peak = jnp.max(scores, axis=-1, keepdims=True)
                weight = jnp.exp2((scores - peak) * factor)
                total = jnp.sum(weight, axis=-1, keepdims=True)
                mixed = jnp.dot(
                    weight.astype(jnp.bfloat16), chosen(values, span),
                    preferred_element_type=jnp.float32,
                )
                mixed = (mixed / total).astype(jnp.bfloat16)
                for g in range(per_kv):
                    to[block, slot, :, :, spans[g]] = mixed[g * rows:(g + 1) * rows].reshape(
                        lanes, share, HEAD
                    )

    def give_back(step, copy, source, block, owner, done, skip, wide):
        for turn in range(1, lanes):
            copy(block, lax.rem(lane + turn, lanes), owner, lane, source).start()

        @pl.when(step > 0)
        def _():
            copy(block, lane, owner, lane, source).start()

        @pl.when(step == 0)
        def _():
            start = pl.multiple_of(lane * width + skip, HEAD)
            stage[pl.ds(owner * CAPC, CAPC), :, pl.ds(start, wide)] = done[block, :, lane]

    def far_work(step, carry):
        source = lax.rem(me + groups - offset_of(lax.rem(step + groups - 1, groups)), groups)

        @pl.when(step > 0)
        def _():
            for copy in q_copies(source, source, source):
                copy.wait_recv()

        attend(q_in, sel_in, res, source, k_ref, v_ref, moved, kv_local - moved)
        give_back(step, r_copy, source, source, me, res, wide_near, width - wide_near)
        return carry

    def near_work(kind, keys, values, owner):
        def body(step, carry):
            seat = lax.rem(spot + step, half)
            block = seat + half * kind

            @pl.when(step > 0)
            def _():
                for copy in n_copies(block, block, base + seat):
                    copy.wait_recv()

            attend(n_in, ns_in, n_res, block, keys, values, 0, moved)
            give_back(step, nr_copy, base + seat, block, owner, n_res, 0, wide_near)
            return carry

        lax.fori_loop(0, half, body, 0)

    if moved:
        near_work(0, k_ref, v_ref, me)
    lax.fori_loop(0, groups, far_work, 0)
    if moved:
        for copy in kv_copies():
            copy.wait_recv()
        near_work(1, k_far, v_far, mirror)

    def returned(step, copy, block, owner, device):
        @pl.when(step > 0)
        def _():
            copy(block, lane, owner, lane, device).wait_send()
            copy(block, lane, owner, lane, device).wait_recv()

        for turn in range(1, lanes):
            piece = lax.rem(lane + turn, lanes)
            copy(block, piece, owner, piece, device).wait_send()
            copy(block, piece, owner, piece, device).wait_recv()

    def far_settle(step, carry):
        other = lax.rem(me + step, groups)

        @pl.when(step > 0)
        def _():
            for copy in q_copies(other, me, other):
                copy.wait_send()

        returned(step, r_copy, other, other, other)
        return carry

    lax.fori_loop(0, groups, far_settle, 0)
    if moved:
        for copy in kv_copies():
            copy.wait_send()

        def near_settle(step, carry):
            seat = lax.rem(spot + step, half)
            for kind in range(2):
                owner = lax.rem(base + half * kind, groups) + seat

                @pl.when(step > 0)
                def _():
                    for copy in n_copies(owner, owner, base + seat):
                        copy.wait_send()

                returned(step, nr_copy, seat + half * kind, owner, base + seat)
            return carry

        lax.fori_loop(0, half, near_settle, 0)

    def deliver(item, carry):
        found = stage[dest_ref[item]].astype(jnp.float32)
        position = lane * share + lax.broadcasted_iota(jnp.int32, found.shape, 0)
        out_ref[item] = jnp.where(position < length_ref[item], found, 0.0).astype(jnp.bfloat16)
        return carry

    lax.fori_loop(0, held, deliver, 0)


def local(groups, lanes, queries, prefix_keys, prefix_values, slot_of_prompt, prompt_of, lengths):
    held, rows, width = queries.shape
    cached, prefix, kv_width = prefix_keys.shape
    share = rows // lanes
    kv_local = kv_width // HEAD
    moved = kv_local // 2 if groups % 2 == 0 and groups >= 4 else 0
    wide_near = moved * (width // kv_local)
    wide = width - wide_near
    cos, sin = rotary_tables(prefix, rows)
    cache_rows = slot_of_prompt[prompt_of]
    owner = cache_rows // cached
    serial = jnp.arange(held)
    earlier = (owner[None, :] == owner[:, None]) & (serial[None, :] < serial[:, None])
    destination = owner * CAPC + jnp.sum(earlier.astype(jnp.int32), axis=1)
    matches = destination[None, :] == jnp.arange(groups * CAPC)[:, None]
    source = jnp.sum(jnp.where(matches, serial[None, :], 0), axis=1)
    tags = jnp.sum(jnp.where(matches, (cache_rows % cached)[None, :], 0), axis=1)
    smem = pl.BlockSpec(memory_space=pltpu.SMEM)
    vmem = pl.BlockSpec(memory_space=pltpu.VMEM)
    dma = pltpu.SemaphoreType.DMA
    bf16 = jnp.bfloat16

    def exchange(features):
        return [
            pltpu.VMEM((groups, CAPC, rows, features), bf16),
            pltpu.VMEM((groups, CAPC, rows, features), bf16),
            pltpu.VMEM((groups, CAPC * cached, TILE, HEAD), bf16),
            pltpu.VMEM((groups, CAPC * cached, TILE, HEAD), bf16),
            pltpu.VMEM((groups, CAPC, lanes, share, features), bf16),
        ]

    semaphores = [
        dma((groups,)), dma((groups,)),
        dma((groups,)), dma((groups,)),
        dma((groups, lanes)), dma((groups, lanes)),
    ]
    scratch = [
        *exchange(wide),
        pltpu.VMEM((groups * CAPC, share, width * lanes), bf16),
        *semaphores,
    ]
    if moved:
        scratch += [
            *exchange(wide_near),
            pltpu.VMEM((cached, prefix, moved * HEAD), bf16),
            pltpu.VMEM((cached, prefix, moved * HEAD), bf16),
            *semaphores,
            dma((2,)), dma((2,)),
        ]
    return pl.pallas_call(
        functools.partial(kernel, groups, lanes, moved),
        out_shape=jax.ShapeDtypeStruct((held, share, width * lanes), bf16),
        in_specs=[smem] * 4 + [vmem] * 5,
        out_specs=vmem,
        scratch_shapes=scratch,
        compiler_params=pltpu.CompilerParams(collective_id=0, has_side_effects=True),
        name="routed_prefix_attention",
    )(
        source.astype(jnp.int32), tags.astype(jnp.int32), destination.astype(jnp.int32), lengths,
        queries, prefix_keys, prefix_values, jnp.asarray(cos), jnp.asarray(sin),
    )


def solution(mesh):
    placed = (
        P("group", None, "tensor"),
        P("group", None, "tensor"),
        P("group", None, "tensor"),
        P(),
        P("group"),
        P("group"),
    )
    return jax.shard_map(
        functools.partial(local, mesh.shape["group"], mesh.shape["tensor"]),
        mesh=mesh, in_specs=placed, out_specs=P("group", "tensor", None), check_vma=False,
    )
```

profile of v0, /device:TPU:0, one launch (start us, length us, event | category | flops | bytes accessed | tf_op | source)
XLA Modules:
  0.0 122.1 jit_solution(10501373057311168913)
XLA Ops:
  0.0 0.0 copy-start
  0.0 0.7 compare_select_fusion
  0.7 0.0 copy-done
  0.7 0.6 gather_fusion
  1.3 0.2 convert_reduce_fusion
  1.5 0.0 copy-start.1
  1.5 0.6 select_reduce_fusion
  2.2 0.0 copy-done.1
  2.2 117.5 %routed_prefix_attention.1 = bf16[8,16,5120]{2,1,0:T(8,128)(2,1)} custom-call(s32[16]{0:T(128)} %get-tuple-element.6.source_ref, s32[16]{0:T(128)} %get-tuple-element.5.tag_ref, s32[8]{0:T(128)} %copy-done.1, s32[8]{0:T(128)} %length_ref.1, bf16[8,64,1280]{2,1,0:T(8,128)(2,1)} %q_ref.1, bf16[2,1024,256]{2,1,0:T(8,128)(2,1)} %k_ref.1, ...), custom_call_target="tpu_custom_call" | custom-call | tf_op jit(solution)/shard_map/routed_prefix_attention/pallas_call | solution.py:360
  119.7 2.5 %copy.10 = bf16[8,16,5120]{2,1,0:T(8,128)(2,1)} copy(bf16[8,16,5120]{2,1,0:T(8,128)(2,1)} %routed_prefix_attention.1) | data formatting | bytes 2621440
  (3 shorter events, 0.0 us)
Async XLA Ops:
  0.0 0.7 copy-start
  1.5 0.6 copy-start.1
where the time goes:
time: 124 us; the launch traced here: 122 us
  Pallas kernels  117 us (94%)
  local copies, waits for them, and re-layouts  3.11 us (3%)
  other arithmetic  1.51 us (1%)
    pallas_call x1, Pallas kernels, local(): pl.pallas_call(functools.partial(kernel, groups, lanes, moved), out_shape...  117 us

commit v1 on v0

--- a/solution.py
+++ b/solution.py
@@ -14,7 +14,11 @@
 CAPC = 2
 ROTARY_BASE = 1000000.0
 TILE = 16
+UNIT = 8
+BATCH = 4
+LANES = 128
 MESH = pl.DeviceIdType.MESH
+LEVELS = ((0.625, 0.47), (0.6875, 0.532), (0.75, 0.594), (0.875, 0.6875), (1.0, 1.0))
 
 
 def rotary_tables(first_position, rows):
@@ -31,7 +35,7 @@
     )
 
 
-def kernel(
+def padded_kernel(
     groups, lanes, moved,
     source_ref, tag_ref, dest_ref, length_ref,
     q_ref, k_ref, v_ref, cos_ref, sin_ref,
@@ -308,7 +312,7 @@
     lax.fori_loop(0, held, deliver, 0)
 
 
-def local(groups, lanes, queries, prefix_keys, prefix_values, slot_of_prompt, prompt_of, lengths):
+def padded(groups, lanes, queries, prefix_keys, prefix_values, slot_of_prompt, prompt_of, lengths):
     held, rows, width = queries.shape
     cached, prefix, kv_width = prefix_keys.shape
     share = rows // lanes
@@ -358,7 +362,7 @@
             dma((2,)), dma((2,)),
         ]
     return pl.pallas_call(
-        functools.partial(kernel, groups, lanes, moved),
+        functools.partial(padded_kernel, groups, lanes, moved),
         out_shape=jax.ShapeDtypeStruct((held, share, width * lanes), bf16),
         in_specs=[smem] * 4 + [vmem] * 5,
         out_specs=vmem,
@@ -369,6 +373,524 @@
         source.astype(jnp.int32), tags.astype(jnp.int32), destination.astype(jnp.int32), lengths,
         queries, prefix_keys, prefix_values, jnp.asarray(cos), jnp.asarray(sin),
     )
+
+
+def xor_order(step, plane, planes):
+    half = planes // 2
+    near = lax.div(step, half)
+    side = lax.rem(lax.div(plane, half) + 1 - near, 2)
+    return side * half + lax.rem(lax.rem(plane, half) + step + near, half)
+
+
+def plan_kernel(
+    groups, pair, levels, full, batches,
+    slot_ref, prompt_ref, length_ref,
+    tables_ref,
+    mine, gathered, send, recv,
+):
+    me, lane = lax.axis_index("group"), lax.axis_index("tensor")
+    held = prompt_ref.shape[0]
+    slots = slot_ref.shape[0]
+    planes = groups // pair
+    per_plane = slots // planes
+    total = groups * held
+    full_pair, full_plane = full
+    barrier = pltpu.get_barrier_semaphore()
+
+    def greet(step, carry):
+        pl.semaphore_signal(
+            barrier, inc=1, device_id=(lax.rem(me + step, groups), lane), device_id_type=MESH
+        )
+        return carry
+
+    lax.fori_loop(1, groups, greet, 0)
+    lanes1 = lax.broadcasted_iota(jnp.int32, (1, LANES), 1)
+    row = jnp.zeros((1, LANES), jnp.int32)
+    for i in range(held):
+        value = slot_ref[prompt_ref[i]] * LANES + length_ref[i]
+        row = jnp.where(lanes1 == me * held + i, value, row)
+    mine[...] = row
+    gathered[me] = row
+    pl.semaphore_wait(barrier, groups - 1)
+
+    def copy(there, device):
+        return pltpu.make_async_remote_copy(
+            src_ref=mine, dst_ref=gathered.at[there], send_sem=send.at[device],
+            recv_sem=recv.at[there], device_id=(device, lane), device_id_type=MESH,
+        )
+
+    def push(step, carry):
+        copy(me, lax.rem(me + step, groups)).start()
+        return carry
+
+    lax.fori_loop(1, groups, push, 0)
+
+    def settle(step, carry):
+        other = lax.rem(me + step, groups)
+        copy(other, other).wait_recv()
+        copy(me, other).wait_send()
+        return carry
+
+    lax.fori_loop(1, groups, settle, 0)
+    code = gathered[0]
+    for g in range(1, groups):
+        code = code + gathered[g]
+
+    square = (LANES, LANES)
+    down = lax.broadcasted_iota(jnp.int32, square, 0)
+    across = lax.broadcasted_iota(jnp.int32, square, 1)
+    eye = down == across
+
+    def to_column(values):
+        return jnp.sum(jnp.where(eye, jnp.broadcast_to(values, square), 0), axis=1, keepdims=True)
+
+    def to_row(values):
+        return jnp.sum(jnp.where(eye, jnp.broadcast_to(values, square), 0), axis=0, keepdims=True)
+
+    def facts(values, index):
+        live = index < total
+        length = values % LANES
+        slot = values // LANES
+        count = jnp.where(live, (length + UNIT - 1) // UNIT, 0)
+        return count, slot, slot // per_plane, index // held, index // (held * pair)
+
+    col = to_column(code)
+    down1 = lax.broadcasted_iota(jnp.int32, (LANES, 1), 0)
+    count_r, slot_r, to_r, from_r, plane_r = facts(code, lanes1)
+    count_c, slot_c, to_c, from_c, plane_c = facts(col, down1)
+    weight = jnp.broadcast_to(count_c, square)
+    earlier = (down < across) & (to_c == to_r)
+
+    def rank(mask):
+        return jnp.sum(jnp.where(mask, weight, 0), axis=0, keepdims=True)
+
+    base1 = rank(earlier & (from_c == from_r))
+    base2 = rank(earlier & (plane_c == plane_r))
+    within = rank(earlier & (plane_c == plane_r) & (slot_c == slot_r))
+    key_r = plane_r * slots + slot_r
+    number = jnp.sum(
+        jnp.where(down1 == key_r, jnp.broadcast_to(count_r, square), 0), axis=1, keepdims=True
+    )
+    need = (number + BATCH - 1) // BATCH
+    need_r = to_row(need)
+    first = jnp.sum(
+        jnp.where(
+            (down // per_plane == across // per_plane) & (across < down),
+            jnp.broadcast_to(need_r, square), 0,
+        ),
+        axis=1, keepdims=True,
+    )
+    first_of = jnp.sum(
+        jnp.where(down1 == key_r, jnp.broadcast_to(first, square), 0), axis=0, keepdims=True
+    )
+    place = first_of * BATCH + within
+    base1_c, base2_c, place_c = to_column(base1), to_column(base2), to_column(place)
+
+    z = me // pair
+    wide1 = jnp.max(jnp.where(lanes1 < total, base1 + count_r, 0), keepdims=True)
+    wide2 = jnp.max(jnp.where(lanes1 < total, base2 + count_r, 0), keepdims=True)
+    level = jnp.zeros((1, 1), jnp.int32)
+    for cap1, cap2 in levels[:-1]:
+        level = level + jnp.where((wide1 > cap1) | (wide2 > cap2), 1, 0)
+    tables_ref[pl.ds(0, 1), :] = jnp.broadcast_to(level, (1, LANES))
+    tables_ref[pl.ds(1, 1), :] = code
+    tables_ref[pl.ds(2, 1), :] = to_r * full_plane + base2
+
+    def pick(mask, start_c, value_c, index):
+        hit = mask & (index >= start_c) & (index < start_c + count_c)
+        return jnp.sum(jnp.where(hit, value_c + index, 0), axis=0, keepdims=True)
+
+    for plane in range(planes):
+        tables_ref[pl.ds(3 + plane, 1), :] = pick(
+            (from_c == me) & (to_c == plane), base1_c,
+            lax.rem(down1, held) * (full_pair // (CAPC * pair)) - base1_c, lanes1,
+        )
+        here = (plane_c == plane) & (to_c == z)
+        tables_ref[pl.ds(3 + planes + plane, 1), :] = pick(
+            here, place_c, lax.rem(from_c, pair) * full_pair + base1_c - place_c, lanes1
+        )
+        tables_ref[pl.ds(3 + 2 * planes + plane, 1), :] = pick(
+            here, base2_c, place_c - base2_c, lanes1
+        )
+        starts = (
+            (down1 // slots == plane) & (lax.rem(down1, slots) // per_plane == z)
+            & (lanes1 >= first) & (lanes1 < first + need)
+        )
+        tables_ref[pl.ds(3 + 3 * planes + plane, 1), :] = jnp.sum(
+            jnp.where(starts, lax.rem(down1, per_plane), 0), axis=0, keepdims=True
+        )
+
+
+def packed_kernel(
+    groups, lanes, pair, full, cap1, cap2, batches,
+    tables,
+    q_ref, k_ref, v_ref, cos_ref, sin_ref,
+    out_ref,
+    q_out, q_in, k_all, v_all, results, r_out_a, r_out_b, r_in_a, r_in_b, stage_a, stage_b,
+    q_send, q_recv, kv_send, kv_recv, kv_here,
+    ra_send, ra_recv, rb_send, rb_recv, fa_send, fa_recv, fb_send, fb_recv,
+):
+    me, lane = lax.axis_index("group"), lax.axis_index("tensor")
+    planes = groups // pair
+    z, x = lax.div(me, pair), lax.rem(me, pair)
+    partner = z * pair + 1 - x
+    cached, prefix, _ = k_ref.shape
+    units, _, width = q_ref.shape
+    wide = width // pair
+    per_kv = wide // HEAD
+    turns = cos_ref.shape[0]
+    held = units // turns
+    share = turns // lanes
+    full_pair, full_plane = full
+    factor = math.log2(math.e) / math.sqrt(HEAD)
+    wide_a = r_in_a.shape[-1]
+    wide_b = wide - wide_a
+    send_row, comp_row, ret_row, slot_row = 3, 3 + planes, 3 + 2 * planes, 3 + 3 * planes
+
+    barrier = pltpu.get_barrier_semaphore()
+
+    def greet(step, carry):
+        pl.semaphore_signal(
+            barrier, inc=1, device_id=(lax.rem(me + step, groups), lane), device_id_type=MESH
+        )
+        return carry
+
+    lax.fori_loop(1, groups, greet, 0)
+    for turn in range(1, lanes):
+        for j in range(pair):
+            pl.semaphore_signal(
+                barrier, inc=1,
+                device_id=(z * pair + j, lax.rem(lane + turn, lanes)), device_id_type=MESH,
+            )
+
+    def span_of(j):
+        return pl.ds(pl.multiple_of(j * HEAD, HEAD), HEAD)
+
+    own = [
+        pltpu.make_async_copy(
+            ref.at[:, :, span_of(x)], full_ref.at[pl.ds(x * cached, cached)], kv_here.at[i]
+        )
+        for i, (ref, full_ref) in enumerate(((k_ref, k_all), (v_ref, v_all)))
+    ]
+    for copy in own:
+        copy.start()
+
+    def remote(src, dst, send_sem, recv_sem, group, to_lane):
+        return pltpu.make_async_remote_copy(
+            src_ref=src, dst_ref=dst, send_sem=send_sem, recv_sem=recv_sem,
+            device_id=(group, to_lane), device_id_type=MESH,
+        )
+
+    def kv_copies(half):
+        return [
+            remote(
+                ref.at[:, :, span_of(1 - x)], full_ref.at[pl.ds(half * cached, cached)],
+                kv_send.at[i], kv_recv.at[i], partner, lane,
+            )
+            for i, (ref, full_ref) in enumerate(((k_ref, k_all), (v_ref, v_all)))
+        ]
+
+    def q_copy(plane, j, source, device):
+        return remote(
+            q_out.at[plane, j], q_in.at[source], q_send.at[plane, j], q_recv.at[source],
+            device, lane,
+        )
+
+    def fill(plane):
+        def one(k, carry):
+            index = tables[send_row + plane, k]
+            turn = lax.rem(index, turns)
+            cos, sin = cos_ref[turn], sin_ref[turn]
+            block = q_ref[index].astype(jnp.float32)
+            for j in range(pair):
+                parts = []
+                for g in range(per_kv):
+                    head = j * per_kv + g
+                    part = block[:, head * HEAD:(head + 1) * HEAD]
+                    turned = part * cos + pltpu.roll(part, HEAD // 2, 1) * sin
+                    parts.append(turned.astype(jnp.bfloat16))
+                q_out[plane, j, k] = jnp.concatenate(parts, axis=1)
+            return carry
+
+        lax.fori_loop(0, cap1, one, 0, unroll=2)
+
+    def dispatch(step, carry):
+        plane = xor_order(step, z, planes)
+        fill(plane)
+
+        @pl.when(step == 0)
+        def _():
+            pl.semaphore_wait(barrier, groups - 1 + pair * (lanes - 1))
+
+        for j in range(pair):
+            @pl.when((step < planes - 1) | (j != x))
+            def _():
+                q_copy(plane, j, me, plane * pair + j).start()
+        return carry
+
+    lax.fori_loop(0, planes, dispatch, 0)
+    for copy in kv_copies(x):
+        copy.start()
+    q_in[me] = q_out[z, x]
+    for copy in own:
+        copy.wait()
+
+    def arrive(step, carry):
+        other = lax.rem(me + step, groups)
+        q_copy(z, x, other, other).wait_recv()
+        return carry
+
+    lax.fori_loop(1, groups, arrive, 0)
+    for copy in kv_copies(1 - x):
+        copy.wait_recv()
+
+    def ra_copy(plane, at, device):
+        return remote(
+            r_out_a.at[plane], r_in_a.at[at], ra_send.at[plane], ra_recv.at[at], device, lane
+        )
+
+    def rb_copy(plane, at, device):
+        return remote(
+            r_out_b.at[plane], r_in_b.at[at], rb_send.at[plane], rb_recv.at[at], device, lane
+        )
+
+    def work(step, carry):
+        plane = xor_order(step, z, planes)
+
+        def batch(b, inner):
+            slot = tables[slot_row + plane, b]
+            blocks = []
+            for i in range(BATCH):
+                index = tables[comp_row + plane, b * BATCH + i]
+                source = plane * pair + lax.div(index, full_pair)
+                blocks.append(q_in[source, lax.rem(index, full_pair)].astype(jnp.float32))
+            query = jnp.concatenate(
+                [block[:, g * HEAD:(g + 1) * HEAD] for g in range(per_kv) for block in blocks],
+                axis=0,
+            ).astype(jnp.bfloat16)
+            scores = lax.dot_general(
+                query, k_all[slot], (((1,), (1,)), ((), ())), preferred_element_type=jnp.float32
+            )
+            peak = jnp.max(scores, axis=-1, keepdims=True)
+            weight = jnp.exp2((scores - peak) * factor)
+            total = jnp.sum(weight, axis=-1, keepdims=True)
+            mixed = jnp.dot(
+                weight.astype(jnp.bfloat16), v_all[slot], preferred_element_type=jnp.float32
+            ) / total
+            for i in range(BATCH):
+                results[b * BATCH + i] = jnp.concatenate(
+                    [
+                        mixed[(g * BATCH + i) * UNIT:(g * BATCH + i + 1) * UNIT]
+                        for g in range(per_kv)
+                    ],
+                    axis=1,
+                ).astype(jnp.bfloat16)
+            return inner
+
+        lax.fori_loop(0, batches, batch, 0)
+
+        def pack(k, inner):
+            found = results[tables[ret_row + plane, k]]
+            r_out_a[plane, k] = found[:, :wide_a]
+            r_out_b[plane, k] = found[:, wide_a:]
+            return inner
+
+        lax.fori_loop(0, cap2, pack, 0, unroll=2)
+
+        @pl.when(step < planes - 1)
+        def _():
+            ra_copy(plane, z, plane * pair + x).start()
+        return carry
+
+    lax.fori_loop(0, planes, work, 0)
+
+    def second(step, carry):
+        plane = xor_order(step, z, planes)
+        rb_copy(plane, z, plane * pair + x).start()
+        return carry
+
+    lax.fori_loop(0, planes - 1, second, 0)
+    r_in_a[z] = r_out_a[z]
+    r_in_b[z] = r_out_b[z]
+
+    start_of = (lane * pair + x) * wide
+
+    def finish(r_copy, r_in, stage, f_send, f_recv, skip, part):
+        def back(step, carry):
+            plane = xor_order(step, z, planes)
+            r_copy(plane, plane, plane * pair + x).wait_recv()
+            return carry
+
+        lax.fori_loop(0, planes - 1, back, 0)
+
+        def spread(step, carry):
+            to_lane = lax.rem(lane + lax.div(step + 1, pair), lanes)
+            to_x = lax.rem(x + step + 1, pair)
+
+            def one(i, inner):
+                item = (z * pair + to_x) * held + i
+                entry = tables[2, item]
+                length = lax.rem(tables[1, item], LANES)
+                source, rank = lax.div(entry, full_plane), lax.rem(entry, full_plane)
+                for s in range(share):
+                    unit = to_lane * share + s
+                    found = r_in[source, jnp.minimum(rank + unit, cap2 - 1)].astype(jnp.float32)
+                    row = unit * UNIT + lax.broadcasted_iota(jnp.int32, found.shape, 0)
+                    stage[to_x, to_lane, i * share + s] = jnp.where(
+                        row < length, found, 0.0
+                    ).astype(jnp.bfloat16)
+                return inner
+
+            lax.fori_loop(0, held, one, 0, unroll=2)
+
+            @pl.when(step < pair * lanes - 1)
+            def _():
+                final(to_x, to_lane, x, lane, to_x, to_lane).start()
+            return carry
+
+        def final(at_x, at_lane, from_x, from_lane, to_x, to_lane):
+            start = pl.multiple_of((from_lane * pair + from_x) * wide + skip, HEAD)
+            return remote(
+                stage.at[at_x, at_lane], out_ref.at[:, :, pl.ds(start, part)],
+                f_send.at[at_x, at_lane], f_recv.at[from_x, from_lane],
+                z * pair + to_x, to_lane,
+            )
+
+        lax.fori_loop(0, pair * lanes, spread, 0)
+        start = pl.multiple_of(start_of + skip, HEAD)
+        out_ref[:, :, pl.ds(start, part)] = stage[x, lane]
+        return final
+
+    final_a = finish(ra_copy, r_in_a, stage_a, fa_send, fa_recv, 0, wide_a)
+    final_b = finish(rb_copy, r_in_b, stage_b, fb_send, fb_recv, wide_a, wide_b)
+
+    def drain(step, carry):
+        to_lane = lax.rem(lane + lax.div(step + 1, pair), lanes)
+        to_x = lax.rem(x + step + 1, pair)
+        for final in (final_a, final_b):
+            final(to_x, to_lane, to_x, to_lane, to_x, to_lane).wait_recv()
+            final(to_x, to_lane, x, lane, to_x, to_lane).wait_send()
+        return carry
+
+    lax.fori_loop(0, pair * lanes - 1, drain, 0)
+
+    def settle(step, carry):
+        plane = xor_order(step, z, planes)
+        for j in range(pair):
+            @pl.when((step < planes - 1) | (j != x))
+            def _():
+                q_copy(plane, j, me, plane * pair + j).wait_send()
+
+        @pl.when(step < planes - 1)
+        def _():
+            ra_copy(plane, z, plane * pair + x).wait_send()
+            rb_copy(plane, z, plane * pair + x).wait_send()
+        return carry
+
+    lax.fori_loop(0, planes, settle, 0)
+    for copy in kv_copies(x):
+        copy.wait_send()
+
+
+def packed(groups, lanes, queries, prefix_keys, prefix_values, slot_of_prompt, prompt_of, lengths):
+    held, rows, width = queries.shape
+    cached, prefix, kv_width = prefix_keys.shape
+    pair = kv_width // HEAD
+    planes = groups // pair
+    turns = rows // UNIT
+    full_pair = CAPC * pair * turns
+    full_plane = full_pair * pair
+    slots = cached * pair
+    share = turns // lanes
+    wide = width // pair
+    per_kv = wide // HEAD
+    wide_a = (per_kv + 1) // 2 * HEAD
+    wide_b = wide - wide_a
+    levels = [
+        (math.ceil(full_pair * one), math.ceil(full_plane * two)) for one, two in LEVELS
+    ]
+    batch_caps = [(cap2 + slots * (BATCH - 1)) // BATCH for _, cap2 in levels]
+    smem = pl.BlockSpec(memory_space=pltpu.SMEM)
+    vmem = pl.BlockSpec(memory_space=pltpu.VMEM)
+    dma = pltpu.SemaphoreType.DMA
+    bf16 = jnp.bfloat16
+    table_rows = -(-(3 + 4 * planes) // 8) * 8
+    full = (full_pair, full_plane)
+    tables = pl.pallas_call(
+        functools.partial(plan_kernel, groups, pair, levels, full, batch_caps),
+        out_shape=jax.ShapeDtypeStruct((table_rows, LANES), jnp.int32),
+        in_specs=[smem] * 3,
+        out_specs=vmem,
+        scratch_shapes=[
+            pltpu.VMEM((1, LANES), jnp.int32),
+            pltpu.VMEM((groups, 1, LANES), jnp.int32),
+            dma((groups,)), dma((groups,)),
+        ],
+        compiler_params=pltpu.CompilerParams(collective_id=1, has_side_effects=True),
+        name="routing_tables",
+    )(slot_of_prompt, prompt_of, lengths)
+
+    cos, sin = rotary_tables(prefix, rows)
+    shaped = (turns, UNIT, HEAD)
+    operands = (
+        tables, queries.reshape(held * turns, UNIT, width), prefix_keys, prefix_values,
+        jnp.asarray(cos.reshape(shaped)), jnp.asarray(sin.reshape(shaped)),
+    )
+
+    def branch(level):
+        cap1, cap2 = levels[level]
+        batches = batch_caps[level]
+
+        def run(*values):
+            return pl.pallas_call(
+                functools.partial(packed_kernel, groups, lanes, pair, full, cap1, cap2, batches),
+                out_shape=jax.ShapeDtypeStruct((held * share, UNIT, width * lanes), bf16),
+                in_specs=[smem] + [vmem] * 5,
+                out_specs=vmem,
+                scratch_shapes=[
+                    pltpu.VMEM((planes, pair, cap1, UNIT, wide), bf16),
+                    pltpu.VMEM((groups, cap1, UNIT, wide), bf16),
+                    pltpu.VMEM((slots, prefix, HEAD), bf16),
+                    pltpu.VMEM((slots, prefix, HEAD), bf16),
+                    pltpu.VMEM((batches * BATCH, UNIT, wide), bf16),
+                    pltpu.VMEM((planes, cap2, UNIT, wide_a), bf16),
+                    pltpu.VMEM((planes, cap2, UNIT, wide_b), bf16),
+                    pltpu.VMEM((planes, cap2, UNIT, wide_a), bf16),
+                    pltpu.VMEM((planes, cap2, UNIT, wide_b), bf16),
+                    pltpu.VMEM((pair, lanes, held * share, UNIT, wide_a), bf16),
+                    pltpu.VMEM((pair, lanes, held * share, UNIT, wide_b), bf16),
+                    dma((planes, pair)), dma((groups,)), dma((2,)), dma((2,)), dma((2,)),
+                    dma((planes,)), dma((planes,)), dma((planes,)), dma((planes,)),
+                    dma((pair, lanes)), dma((pair, lanes)),
+                    dma((pair, lanes)), dma((pair, lanes)),
+                ],
+                compiler_params=pltpu.CompilerParams(
+                    collective_id=2 + level, has_side_effects=True
+                ),
+                name=f"packed_prefix_attention_{level}",
+            )(*values)
+
+        return run
+
+    out = lax.switch(tables[0, 0], [branch(level) for level in range(len(levels))], *operands)
+    return out.reshape(held, share * UNIT, width * lanes)
+
+
+def fits(groups, lanes, queries, prefix_keys):
+    held, rows, width = queries.shape
+    pair = prefix_keys.shape[2] // HEAD
+    if pair != 2 or groups % (2 * pair) or rows % (UNIT * lanes):
+        return False
+    planes = groups // pair
+    spots = planes * planes * pair * prefix_keys.shape[0]
+    full_plane = CAPC * pair * pair * rows // UNIT
+    room = full_plane + pair * prefix_keys.shape[0] * (BATCH - 1)
+    return groups * held <= LANES and spots <= LANES and room <= LANES
+
+
+def local(groups, lanes, queries, prefix_keys, *rest):
+    form = packed if fits(groups, lanes, queries, prefix_keys) else padded
+    return form(groups, lanes, queries, prefix_keys, *rest)
 
 
 def solution(mesh):

time: 124 us -> 109 us (0.88)
  the two profiles are of different devices: /device:TPU:0 before, /device:TPU:13 now
where the time goes in v1:
time: 109 us
  Pallas kernels  107 us (98%)
  local copies, waits for them, and re-layouts  1.57 us (1%)
    pallas_call x1, Pallas kernels, run(): pl.pallas_call(functools.partial(packed_kernel, groups, lanes, pair, full...  99.7 us
    pallas_call x1, Pallas kernels, packed(): pl.pallas_call(functools.partial(plan_kernel, groups, pair, levels, full,...  6.81 us

profile of v1, /device:TPU:13, one launch (start us, length us, event | category | flops | bytes accessed | tf_op | source)
XLA Modules:
  0.0 108.8 jit_solution(8907331801169844395)
XLA Ops:
  0.0 6.8 %routing_tables.1 = s32[24,128]{1,0:T(8,128)S(1)} custom-call(s32[16]{0:T(128)} %slot_ref.1, s32[8]{0:T(128)} %prompt_ref.1, s32[8]{0:T(128)} %length_ref.1), custom_call_target="tpu_custom_call" | custom-call | tf_op jit(solution)/shard_map/routing_tables/pallas_call | solution.py:819
  6.8 0.5 slice.3
  8.0 99.8 %conditional.1 = (bf16[8,16,5120]{2,1,0:T(8,128)(2,1)S(1)}) conditional(s32[]{:T(128)} %bitcast.5, (s32[24,128]{1,0:T(8,128)S(1)}, bf16[64,8,1280]{2,1,0:T(8,128)(2,1)}, bf16[2,1024,256]{2,1,0:T(8,128)(2,1)}, bf16[2,1024,256]{2,1,0:T(8,128)(2,1)}, f32[8,8,128]{2,1,0:T(8,128)}, ...), branch_computations={%region_0.0_spmd, %region_1.0_spmd, %region_2.0_spmd, %region_3.0_... | conditional | bytes 8 | solution.py:875
  8.0 99.7 %packed_prefix_attention_1.1 = bf16[16,8,5120]{2,1,0:T(8,128)(2,1)S(1)} custom-call(s32[24,128]{1,0:T(8,128)S(1)} %get-tuple-element.78.tables, bf16[64,8,1280]{2,1,0:T(8,128)(2,1)} %get-tuple-element.79.q_ref, bf16[2,1024,256]{2,1,0:T(8,128)(2,1)} %get-tuple-element.80.k_ref, bf16[2,1024,256]{2,1,0:T(8,128)(2,1)} %get-tuple-element.81.v_ref, ...), custom_call_target="tpu_custom_call" | custom-call | tf_op jit(solution)/shard_map/cond/branch_1_fun/packed_prefix_attention_1/pallas_call | solution.py:845
  107.8 1.1 copy.20
